TPU v7x, 32 devices: a whole 2x2x4 slice. The times are simulated.
32 devices in a mesh: frame: 4 (over z), height: 4 (over y, x), dp: 2 (over core).
Axes of the slice: x: 2, y: 2, z: 4, core: 2. Of those that a mesh axis runs over, the one named last changes fastest.
Arguments:
- clip_latents: bfloat16 [2, 8, 64, 16, 320], P('dp', 'frame', 'height'), may hold values from -6 to 6
- out_grad: bfloat16 [2, 8, 64, 16, 320], P('dp', 'frame', 'height'), may hold values from -6 to 6
- box_mask: int32 [2, 8, 64, 16], P('dp', 'frame', 'height'), may hold values from 0 to 1, as said below
- attn_weights: bfloat16 [1280, 320], replicated, may hold values from -0.3125 to 0.3125
- conv_weights: bfloat16 [2880, 320], replicated, may hold values from -0.109375 to 0.109375
- time_bias: float32 [5, 8, 8], replicated, may hold values from -4 to 250
Outputs:
- grad_input: bfloat16 [2, 8, 64, 16, 320], P('dp', 'frame', 'height')
- grad_attn: float32 [1280, 320], P(('frame', 'height', 'dp'))
- grad_conv: float32 [2880, 320], P(('height', 'dp'))
Inputs may be any that keep to these rules, and one draw needn't show every extreme that they name: Each frame of each clip has one grounding box: box_mask is 1 on a rectangle of 16 to 32 rows and 4 to 8 columns, 0 elsewhere.
All inputs are finite; a program needn't handle non-finite values.
Results may differ from a plain program's by a relative error of at most 0.025.
Values may be sent and summed in bfloat16 or wider, within the bound.
No kernel may reach another device: no remote copies, remote signals or barrier semaphores. Data moves between devices by JAX's collectives and lax.ppermute only.
A program may use at most 64 MiB of HBM per device.

v0:
```python
import jax
import jax.numpy as jnp
from jax import lax
from jax.sharding import PartitionSpec as P

ground_bias = 2.0


def padded_2(block, sides, width):
    for axis, dim in sides:
        count = lax.axis_size(axis)
        forward = [(i, i + 1) for i in range(count - 1)]
        backward = [(target, source) for source, target in forward]
        low = lax.ppermute(
            lax.slice_in_dim(block, block.shape[dim] - width, None, axis=dim), axis, forward
        )
        high = lax.ppermute(lax.slice_in_dim(block, 0, width, axis=dim), axis, backward)
        block = jnp.concatenate([low, block, high], axis=dim)
    return block


def silu_slope(value):
    sig = jax.nn.sigmoid(value)
    return sig * (1.0 + value * (1.0 - sig))


def project(matrix, weight):
    flat_rows = matrix.reshape(-1, matrix.shape[-1])
    result = jnp.dot(flat_rows, weight, preferred_element_type=jnp.float32)
    return result.reshape(matrix.shape[:-1] + (weight.shape[1],))


def project_back(matrix, weight):
    flat_rows = matrix.reshape(-1, matrix.shape[-1])
    result = lax.dot_general(
        flat_rows, weight, (((1,), (1,)), ((), ())), preferred_element_type=jnp.float32
    )
    return result.reshape(matrix.shape[:-1] + (weight.shape[0],))


def cross(left, right):
    left_rows = left.reshape(-1, left.shape[-1])
    right_rows = right.reshape(-1, right.shape[-1])
    return lax.dot_general(
        left_rows, right_rows, (((0,), (0,)), ((), ())), preferred_element_type=jnp.float32
    )


def body(clip_latents, out_grad, box_mask, attn_weights, conv_weights, time_bias):
    clip_count, frame_count, row_count, col_count, channels = clip_latents.shape
    head_count = time_bias.shape[0]
    all_frames = time_bias.shape[1]
    head_size = channels // head_count
    pixels = row_count * col_count
    scaling = head_size ** (-0.5)
    w_query = attn_weights[:channels]
    w_key = attn_weights[channels : 2 * channels]
    w_value = attn_weights[2 * channels : 3 * channels]
    w_out = attn_weights[3 * channels :]
    flat_x = clip_latents.reshape(clip_count, frame_count, pixels, channels)
    flat_marks = box_mask.reshape(clip_count, frame_count, pixels).astype(jnp.bfloat16)
    latents_t, marks_t = (
        lax.all_to_all(flat_x, "frame", split_axis=2, concat_axis=1, tiled=True),
        lax.all_to_all(flat_marks, "frame", split_axis=2, concat_axis=1, tiled=True),
    )
    query_t = project(latents_t, w_query).astype(jnp.bfloat16)
    key_t = project(latents_t, w_key).astype(jnp.bfloat16)
    value_t = project(latents_t, w_value).astype(jnp.bfloat16)
    column_tokens = query_t.shape[2]
    head_shape = (clip_count, all_frames, column_tokens, head_count, head_size)
    qh = query_t.reshape(head_shape)
    kh = key_t.reshape(head_shape)
    vh = value_t.reshape(head_shape)
    mark_bias = ground_bias * jnp.transpose(marks_t.astype(jnp.float32), (0, 2, 1))
    score_bias = time_bias[None, None] + mark_bias[:, :, None, None, :]
    scores = (
        jnp.einsum("ctnhd,cunhd->cnhtu", qh, kh, preferred_element_type=jnp.float32) * scaling
        + score_bias
    )
    prob_full = jax.nn.softmax(scores, axis=-1)
    prob_half = prob_full.astype(jnp.bfloat16)
    mixed_t = jnp.einsum(
        "cnhtu,cunhd->ctnhd", prob_half, vh, preferred_element_type=jnp.float32
    ).astype(jnp.bfloat16)
    mixed_t = mixed_t.reshape(clip_count, all_frames, column_tokens, channels)
    mixed_rows = lax.all_to_all(mixed_t, "frame", split_axis=1, concat_axis=2, tiled=True)
    residual = (flat_x.astype(jnp.float32) + project(mixed_rows, w_out)).astype(jnp.bfloat16)
    activated = jax.nn.silu(residual.astype(jnp.float32)).astype(jnp.bfloat16)
    out_flat = out_grad.reshape(clip_count, frame_count, pixels, channels)
    stacked = jnp.concatenate([activated, out_flat], axis=-1).reshape(
        clip_count, frame_count, row_count, col_count, 2 * channels
    )
    padded = padded_2(stacked, (("height", 2),), 1)
    padded = jnp.pad(padded, ((0, 0), (0, 0), (0, 0), (1, 1), (0, 0)))
    act_pad = padded[..., :channels]
    grad_pad = padded[..., channels:]
    out_rows = out_grad.reshape(-1, channels)
    delta_sum = jnp.zeros((out_rows.shape[0], channels), jnp.float32)
    conv_terms = []
    for row_step in (-1, 0, 1):
        for col_step in (-1, 0, 1):
            tap_index = 3 * (row_step + 1) + col_step + 1
            tap_weight = conv_weights[tap_index * channels : (tap_index + 1) * channels]
            shifted = grad_pad[
                :,
                :,
                1 - row_step : 1 - row_step + row_count,
                1 - col_step : 1 - col_step + col_count,
                :,
            ]
            delta_sum = delta_sum + project_back(shifted.reshape(-1, channels), tap_weight)
            moved_rows = act_pad[
                :,
                :,
                1 + row_step : 1 + row_step + row_count,
                1 + col_step : 1 + col_step + col_count,
                :,
            ]
            conv_terms.append(cross(moved_rows, out_rows))
    residual_flat = residual.reshape(-1, channels).astype(jnp.float32)
    upstream = (out_rows.astype(jnp.float32) + silu_slope(residual_flat) * delta_sum).astype(
        jnp.bfloat16
    )
    d_mixed = (
        project_back(upstream, w_out)
        .astype(jnp.bfloat16)
        .reshape(clip_count, frame_count, pixels, channels)
    )
    d_mixed_t = lax.all_to_all(d_mixed, "frame", split_axis=2, concat_axis=1, tiled=True)
    dh = d_mixed_t.reshape(head_shape)
    d_prob = jnp.einsum("ctnhd,cunhd->cnhtu", dh, vh, preferred_element_type=jnp.float32)
    row_dot = jnp.sum(prob_full * d_prob, axis=-1, keepdims=True)
    d_scores = (prob_full * (d_prob - row_dot)).astype(jnp.bfloat16)
    column_shape = (clip_count, all_frames, column_tokens, channels)
    d_query = (
        (
            jnp.einsum("cnhtu,cunhd->ctnhd", d_scores, kh, preferred_element_type=jnp.float32)
            * scaling
        )
        .astype(jnp.bfloat16)
        .reshape(column_shape)
    )
    d_key = (
        (
            jnp.einsum("cnhtu,ctnhd->cunhd", d_scores, qh, preferred_element_type=jnp.float32)
            * scaling
        )
        .astype(jnp.bfloat16)
        .reshape(column_shape)
    )
    d_value = (
        jnp.einsum("cnhtu,ctnhd->cunhd", prob_half, dh, preferred_element_type=jnp.float32)
        .astype(jnp.bfloat16)
        .reshape(column_shape)
    )
    d_inputs_t = (
        project_back(d_query, w_query) + project_back(d_key, w_key) + project_back(d_value, w_value)
    ).astype(jnp.bfloat16)
    d_inputs = lax.all_to_all(d_inputs_t, "frame", split_axis=1, concat_axis=2, tiled=True)
    qkv_terms = [cross(latents_t, d_query), cross(latents_t, d_key), cross(latents_t, d_value)]
    grad_rows = (
        upstream.astype(jnp.float32) + d_inputs.reshape(-1, channels).astype(jnp.float32)
    ).astype(jnp.bfloat16)
    grad_input = grad_rows.reshape(clip_latents.shape)
    token_count = (
        clip_count
        * lax.axis_size("dp")
        * frame_count
        * lax.axis_size("frame")
        * pixels
        * lax.axis_size("height")
    )
    grad_scale = float(token_count) ** (-0.5)
    attn_term = jnp.concatenate(qkv_terms + [cross(mixed_rows, upstream)], axis=0) * grad_scale
    grad_attn = lax.psum_scatter(
        attn_term, ("frame", "height", "dp"), scatter_dimension=0, tiled=True
    )
    conv_term = jnp.concatenate(conv_terms, axis=0) * grad_scale
    summed = lax.psum(conv_term.astype(jnp.bfloat16), "frame")
    grad_conv = lax.psum_scatter(summed, ("height", "dp"), scatter_dimension=0, tiled=True).astype(
        jnp.float32
    )
    return (grad_input, grad_attn, grad_conv)


def solution(mesh):
    in_specs = (
        P("dp", "frame", "height", None, None),
        P("dp", "frame", "height", None, None),
        P("dp", "frame", "height", None),
        P(),
        P(),
        P(),
    )
    out_specs = (
        P("dp", "frame", "height", None, None),
        P(("frame", "height", "dp"), None),
        P(("height", "dp"), None),
    )
    return jax.shard_map(body, mesh=mesh, in_specs=in_specs, out_specs=out_specs, check_vma=False)
```

profile of v0, /device:TPU:0, one launch (start us, length us, event | category | flops | bytes accessed | tf_op | source)
XLA Modules:
  0.0 359.6 jit_solution(10459075539410474658)
XLA Ops:
  8.8 6.3 %all-to-all-start.1 = ((bf16[1,2,256]{1,0,2:T(2,128)(2,1)}), bf16[1,2,256]{1,0,2:T(2,128)(2,1)S(1)}, u32[]{:S(2)}, u32[]{:S(2)}) async-start(bf16[1,2,256]{1,0,2:T(2,128)(2,1)} %copy.236), calls=%async_computation.1 | async-start | bytes 262144 | tf_op jit(solution)/shard_map/all_to_all | solution.py:64
  15.2 2.1 copy.224
  17.3 3.9 %all-to-all-done.1 = bf16[1,2,256]{1,0,2:T(2,128)(2,1)S(1)} async-done(((bf16[1,2,256]{1,0,2:T(2,128)(2,1)}), bf16[1,2,256]{1,0,2:T(2,128)(2,1)S(1)}, u32[]{:S(2)}, u32[]{:S(2)}) %all-to-all-start.1) | async-done | bytes 1056 | tf_op jit(solution)/shard_map/all_to_all | solution.py:64
  21.3 3.5 all-to-all-start
  25.1 10.0 %all-to-all-done = bf16[1,2,256,320]{3,1,0,2:T(2,128)(2,1)S(1)} async-done(((bf16[1,2,256,320]{3,1,0,2:T(2,128)(2,1)}), bf16[1,2,256,320]{3,1,0,2:T(2,128)(2,1)S(1)}, u32[]{:S(2)}, u32[]{:S(2)}) %all-to-all-start) | async-done | bytes 327712 | tf_op jit(solution)/shard_map/all_to_all | solution.py:63
  37.6 1.2 copy.233
  39.1 1.2 copy.240
  40.4 3.3 fusion.59
  44.4 2.7 fusion.7
  47.2 1.6 copy.242
  48.8 1.0 copy.243
  49.8 3.6 all-to-all-start.2
  53.4 1.0 copy.246
  54.4 0.9 copy.223
  56.6 6.7 %all-to-all-done.2 = bf16[1,8,64,320]{3,2,0,1:T(8,128)(2,1)S(1)} async-done(((bf16[1,8,64,320]{3,2,0,1:T(8,128)(2,1)}), bf16[1,8,64,320]{3,2,0,1:T(8,128)(2,1)S(1)}, u32[]{:S(2)}, u32[]{:S(2)}) %all-to-all-start.2) | async-done | bytes 327712 | tf_op jit(solution)/shard_map/all_to_all | solution.py:86
  63.3 2.5 multiply_convert_fusion.2
  66.1 1.4 collective-permute-start.1
  67.6 4.7 %collective-permute-start = (bf16[1,2,1,16,640]{4,3,2,1,0:T(8,128)(2,1)S(1)}, bf16[1,2,1,16,640]{4,3,2,1,0:T(8,128)(2,1)S(1)}, u32[]{:S(2)}, u32[]{:S(2)}) collective-permute-start(bf16[1,2,1,16,640]{4,3,2,1,0:T(8,128)(2,1)S(1)} %get-tuple-element.29), channel_id=1, source_target_pairs={{0,2},{2,4},{4,6},{1,3},{3,5},{5,7},{8,10},{10,12},{12,14},{9,11},... | collective-permute-start | bytes 122888 | tf_op jit(solution)/shard_map/ppermute | solution.py:14
  72.8 1.0 collective-permute-done
  75.4 1.2 convolution_bitcast_fusion.8
  77.1 1.2 convolution_bitcast_fusion.7
  78.2 1.2 convolution_bitcast_fusion.6
  79.4 1.2 convolution_bitcast_fusion.5
  80.6 1.2 convolution_bitcast_fusion.3
  81.8 1.2 convolution_bitcast_fusion.2
  83.2 1.2 convolution_bitcast_fusion.1
  84.4 1.2 convolution_bitcast_fusion
  90.3 1.2 convolution_convert_fusion.5
  91.5 1.8 reshape.304
  93.3 2.0 copy.249
  95.3 4.1 %all-to-all-start.3 = ((bf16[1,2,256,320]{3,1,0,2:T(2,128)(2,1)}), bf16[1,2,256,320]{3,1,0,2:T(2,128)(2,1)}, u32[]{:S(2)}, u32[]{:S(2)}) async-start(bf16[1,2,256,320]{3,1,0,2:T(2,128)(2,1)} %copy.249), calls=%async_computation.3 | async-start | bytes 786432 | tf_op jit(solution)/shard_map/all_to_all | solution.py:129
  99.5 4.8 %concatenate.29 = f32[2880,320]{0,1:T(8,128)} concatenate(f32[320,320]{0,1:T(8,128)S(1)} %copy-done.5, f32[320,320]{0,1:T(8,128)} %convolution_bitcast_fusion.7, f32[320,320]{0,1:T(8,128)} %convolution_bitcast_fusion.6, f32[320,320]{0,1:T(8,128)} %convolution_bitcast_fusion.5, f32[320,320]{0,1:T(8,128)S(1)} %convolution_bitcast_fusion.4, f32[320,320]{0,1:T(8,128)} %convolution_bitcast_fusion.3, ...), dimensions={0} | concatenate | bytes 7372800 | tf_op jit(solution)/shard_map/concatenate | solution.py:178
  104.3 3.6 multiply_convert_fusion
  108.9 1.1 fusion.60
  110.0 1.0 copy.250
  111.4 1.2 copy.252
  112.5 2.6 multiply_reduce_fusion
  118.2 1.4 copy.268
  119.6 2.2 reshape_reshape.12
  121.8 1.4 copy.270
  123.2 2.2 reshape_reshape.13
  125.4 2.1 convolution_bitcast_fusion.11
  127.5 1.1 convolution_bitcast_fusion.10
  128.7 1.4 copy.271
  130.0 2.2 reshape_reshape.14
  132.3 2.1 convolution_bitcast_fusion.9
  134.4 1.3 copy.256
  135.7 1.3 copy.259
  137.0 1.3 copy.262
  138.3 1.9 concatenate.28
  140.2 2.5 fusion.34
  142.7 1.3 broadcast_multiply_fusion
  143.9 27.7 %all-reduce.11.cloned.1.call-done = bf16[2880,320]{0,1:T(8,128)(2,1)} async-done(((bf16[2880,320]{0,1:T(8,128)(2,1)}), bf16[2880,320]{0,1:T(8,128)(2,1)}) %all-reduce.11.cloned.1.call-update) | async-done | bytes 1843216
  171.6 1.8 constant_dynamic-slice_fusion
  173.5 1.9 convolution_add_fusion.1
  175.4 1.1 copy-done.2
  176.5 1.2 fusion.17
  177.7 4.9 %all-to-all-start.4 = ((bf16[1,8,64,320]{3,2,0,1:T(8,128)(2,1)}), bf16[1,8,64,320]{3,2,0,1:T(8,128)(2,1)S(1)}, u32[]{:S(2)}, u32[]{:S(2)}) async-start(bf16[1,8,64,320]{3,2,0,1:T(8,128)(2,1)} %fusion.17), calls=%async_computation.4 | async-start | bytes 786432 | tf_op jit(solution)/shard_map/all_to_all | solution.py:159
  182.6 13.3 %all-to-all-done.4 = bf16[1,8,64,320]{3,2,0,1:T(8,128)(2,1)S(1)} async-done(((bf16[1,8,64,320]{3,2,0,1:T(8,128)(2,1)}), bf16[1,8,64,320]{3,2,0,1:T(8,128)(2,1)S(1)}, u32[]{:S(2)}, u32[]{:S(2)}) %all-to-all-start.4) | async-done | bytes 327712 | tf_op jit(solution)/shard_map/all_to_all | solution.py:159
  196.3 0.9 copy.267
  197.2 16.2 %all-reduce.7.cloned.1.call-done = bf16[360,320]{0,1:T(8,128)(2,1)} async-done(((bf16[360,320]{0,1:T(8,128)(2,1)}), bf16[360,320]{0,1:T(8,128)(2,1)}) %all-reduce.7.cloned.1.call-update) | async-done | bytes 230416 | tf_op jit(solution)/shard_map/psum | solution.py:179
  213.4 1.8 convert_element_type.189
  215.1 136.1 %all-reduce.9.cloned.1.call-done = f32[1280,320]{0,1:T(8,128)} async-done(((f32[1280,320]{0,1:T(8,128)}), f32[1280,320]{0,1:T(8,128)}) %all-reduce.9.cloned.1.call-update) | async-done | bytes 1638416
  351.3 1.1 constant_dynamic-slice_fusion.1
  (92 shorter events, 19.3 us)
Async XLA Ops:
  7.2 17.6 %copy-start.17 = (f32[5,8,8]{2,1,0:T(8,128)S(1)}, f32[5,8,8]{2,1,0:T(8,128)}, u32[]{:S(2)}) copy-start(f32[5,8,8]{2,1,0:T(8,128)} %param.11) | copy-start | bytes 3844
  8.8 12.4 %all-to-all-start.1 = ((bf16[1,2,256]{1,0,2:T(2,128)(2,1)}), bf16[1,2,256]{1,0,2:T(2,128)(2,1)S(1)}, u32[]{:S(2)}, u32[]{:S(2)}) async-start(bf16[1,2,256]{1,0,2:T(2,128)(2,1)} %copy.236), calls=%async_computation.1 | async-start | bytes 262144 | tf_op jit(solution)/shard_map/all_to_all | solution.py:64
  17.3 17.9 %copy-start.1 = (bf16[1280,320]{0,1:T(8,128)(2,1)S(1)}, bf16[1280,320]{0,1:T(8,128)(2,1)}, u32[]{:S(2)}) copy-start(bf16[1280,320]{0,1:T(8,128)(2,1)} %param.9) | copy-start | bytes 2457604
  21.3 13.9 %all-to-all-start = ((bf16[1,2,256,320]{3,1,0,2:T(2,128)(2,1)}), bf16[1,2,256,320]{3,1,0,2:T(2,128)(2,1)S(1)}, u32[]{:S(2)}, u32[]{:S(2)}) async-start(bf16[1,2,256,320]{3,1,0,2:T(2,128)(2,1)} %bitcast.2), calls=%async_computation | async-start | bytes 786432 | tf_op jit(solution)/shard_map/all_to_all | solution.py:63
  40.4 4.0 %copy-start.11 = (bf16[8,64,5,64]{3,0,2,1:T(8,128)(2,1)S(1)}, bf16[8,64,5,64]{3,0,2,1:T(8,128)(2,1)}, u32[]{:S(2)}) copy-start(bf16[8,64,5,64]{3,0,2,1:T(8,128)(2,1)} %copy.240) | copy-start | bytes 983044
  43.7 0.7 copy-start.15
  47.2 6.2 %copy-start.6 = (bf16[1,2,16,16,320]{4,3,2,1,0:T(8,128)(2,1)S(1)}, bf16[1,2,16,16,320]{4,3,2,1,0:T(8,128)(2,1)}, u32[]{:S(2)}) copy-start(bf16[1,2,16,16,320]{4,3,2,1,0:T(8,128)(2,1)} %param.6) | copy-start | bytes 983044
  48.8 5.7 %copy-start = (bf16[1,2,16,16,320]{4,3,2,1,0:T(8,128)(2,1)S(1)}, bf16[1,2,16,16,320]{4,3,2,1,0:T(8,128)(2,1)}, u32[]{:S(2)}) copy-start(bf16[1,2,16,16,320]{4,3,2,1,0:T(8,128)(2,1)} %param.7) | copy-start | bytes 983044
  49.8 5.6 %copy-start.18 = (u32[32]{0:T(128)S(1)}, u32[32]{0:T(128)}, u32[]{:S(2)}) copy-start(u32[32]{0:T(128)} %constant.30) | copy-start | bytes 388
  49.8 13.5 %all-to-all-start.2 = ((bf16[1,8,64,320]{3,2,0,1:T(8,128)(2,1)}), bf16[1,8,64,320]{3,2,0,1:T(8,128)(2,1)S(1)}, u32[]{:S(2)}, u32[]{:S(2)}) async-start(bf16[1,8,64,320]{3,2,0,1:T(8,128)(2,1)} %copy.243), calls=%async_computation.2 | async-start | bytes 786432 | tf_op jit(solution)/shard_map/all_to_all | solution.py:86
  63.3 2.5 copy-start.7
  66.0 6.7 %copy-start.12 = (f32[2,256,320]{1,2,0:T(8,128)S(1)}, f32[2,256,320]{1,2,0:T(8,128)}, u32[]{:S(2)}) copy-start(f32[2,256,320]{1,2,0:T(8,128)} %get-tuple-element.34) | copy-start | bytes 1966084
  66.1 6.6 %collective-permute-start.1 = (bf16[1,2,1,16,640]{4,3,2,1,0:T(8,128)(2,1)S(1)}, bf16[1,2,1,16,640]{4,3,2,1,0:T(8,128)(2,1)S(1)}, u32[]{:S(2)}, u32[]{:S(2)}) collective-permute-start(bf16[1,2,1,16,640]{4,3,2,1,0:T(8,128)(2,1)S(1)} %get-tuple-element.30), channel_id=1, source_target_pairs={{2,0},{4,2},{6,4},{3,1},{5,3},{7,5},{10,8},{12,10},{14,12},{11,9},... | collective-permute-start | bytes 122888 | tf_op jit(solution)/shard_map/ppermute | solution.py:17
  67.6 6.2 %collective-permute-start = (bf16[1,2,1,16,640]{4,3,2,1,0:T(8,128)(2,1)S(1)}, bf16[1,2,1,16,640]{4,3,2,1,0:T(8,128)(2,1)S(1)}, u32[]{:S(2)}, u32[]{:S(2)}) collective-permute-start(bf16[1,2,1,16,640]{4,3,2,1,0:T(8,128)(2,1)S(1)} %get-tuple-element.29), channel_id=1, source_target_pairs={{0,2},{2,4},{4,6},{1,3},{3,5},{5,7},{8,10},{10,12},{12,14},{9,11},... | collective-permute-start | bytes 122888 | tf_op jit(solution)/shard_map/ppermute | solution.py:14
  83.2 2.4 copy-start.4
  88.7 1.0 copy-start.14
  90.2 9.2 %copy-start.5 = (f32[320,320]{0,1:T(8,128)S(1)}, f32[320,320]{0,1:T(8,128)}, u32[]{:S(2)}) copy-start(f32[320,320]{0,1:T(8,128)} %convolution_bitcast_fusion.8) | copy-start | bytes 1228804
  95.3 14.7 %all-to-all-start.3 = ((bf16[1,2,256,320]{3,1,0,2:T(2,128)(2,1)}), bf16[1,2,256,320]{3,1,0,2:T(2,128)(2,1)}, u32[]{:S(2)}, u32[]{:S(2)}) async-start(bf16[1,2,256,320]{3,1,0,2:T(2,128)(2,1)} %copy.249), calls=%async_computation.3 | async-start | bytes 786432 | tf_op jit(solution)/shard_map/all_to_all | solution.py:129
  99.4 72.2 %all-reduce.11.cloned.1.call-start = ((), (), s32[]{:S(2)}) async-start(), calls=%async_computation.7 | async-start | bytes 3768320
  107.9 1.0 copy-start.8
  107.9 105.5 %all-reduce.7.cloned.1.call-start = ((), (), s32[]{:S(2)}) async-start(), calls=%async_computation.5 | async-start | bytes 491520 | tf_op jit(solution)/shard_map/psum | solution.py:179
  112.5 2.6 copy-start.9
  112.5 2.6 copy-start.16
  115.5 1.1 copy-start.3
  116.6 1.1 copy-start.13
  125.4 2.1 copy-start.10
  173.4 177.9 %all-reduce.9.cloned.1.call-start = ((), (), s32[]{:S(2)}) async-start(), calls=%async_computation.6 | async-start | bytes 3276800
  175.4 1.1 copy-start.2
  177.7 18.2 %all-to-all-start.4 = ((bf16[1,8,64,320]{3,2,0,1:T(8,128)(2,1)}), bf16[1,8,64,320]{3,2,0,1:T(8,128)(2,1)S(1)}, u32[]{:S(2)}, u32[]{:S(2)}) async-start(bf16[1,8,64,320]{3,2,0,1:T(8,128)(2,1)} %fusion.17), calls=%async_computation.4 | async-start | bytes 786432 | tf_op jit(solution)/shard_map/all_to_all | solution.py:159
Sparse Core Ops, SparseCore 0:
  108.0 63.5 all-reduce.10
  174.5 38.8 all-reduce.6
  218.8 132.4 all-reduce.8
where the time goes:
time: 361 us; the launch traced here: 360 us
  waiting for transfers between devices  215 us (60%)
  local copies, waits for them, and re-layouts  50.6 us (14%)
  matrix products  41.3 us (11%)
  starting transfers between devices  28.9 us (8%)
  between operations  14.9 us (4%)
  other arithmetic  8.95 us (2%)
    unnamed x5, waiting for transfers between devices  164 us
    dot_general x13, matrix products, cross(): lax.dot_general(left_rows, right_rows, (((0,), (0,)), ((), ())), preferre...  16.4 us
    psum x1, waiting for transfers between devices, body(): summed = lax.psum(conv_term.astype(jnp.bfloat16), 'frame')  16.2 us
    all_to_all x1, waiting for transfers between devices, body(): lax.all_to_all(d_inputs_t, 'frame', split_axis=1, concat_axis=2, tiled=True)  13.3 us
    dot_general x13, matrix products, project_back(): lax.dot_general(flat_rows, weight, (((1,), (1,)), ((), ())), preferred_el...  10.9 us
    unnamed x44, local copies, waits for them, and re-layouts  10.5 us
    all_to_all x1, waiting for transfers between devices, body(): lax.all_to_all(flat_x, 'frame', split_axis=2, concat_axis=1, tiled=True)  10 us
  transfers between devices with their start and end apart: 10, of which 8 were waited for; matrix products, arithmetic and copies ran while one was open for 15% of the time, Pallas kernels for 0%

commit v1 on v0

--- a/solution.py
+++ b/solution.py
@@ -156,7 +156,12 @@
     d_inputs_t = (
         project_back(d_query, w_query) + project_back(d_key, w_key) + project_back(d_value, w_value)
     ).astype(jnp.bfloat16)
-    d_inputs = lax.all_to_all(d_inputs_t, "frame", split_axis=1, concat_axis=2, tiled=True)
+    d_inputs = jnp.concatenate(
+        lax.all_to_all(
+            jnp.stack(jnp.split(d_inputs_t, lax.axis_size("frame"), axis=1)), "frame", 0, 0
+        ),
+        axis=2,
+    )
     qkv_terms = [cross(latents_t, d_query), cross(latents_t, d_key), cross(latents_t, d_value)]
     grad_rows = (
         upstream.astype(jnp.float32) + d_inputs.reshape(-1, channels).astype(jnp.float32)

time: 361 us -> 354 us (0.981)
  local copies, waits for them, and re-layouts: 50.6 us -> 41.8 us
  waiting for transfers between devices: 215 us -> 222 us
  matrix products: 41.3 us -> 35.2 us
    psum x1, waiting for transfers between devices: 16.2 us -> 31.4 us  [body(): summed = lax.psum(conv_term.astype(jnp.bfloat16), 'frame')]
    all_to_all x1, waiting for transfers between devices: 13.3 us -> 0.01 us  [body(): lax.all_to_all(jnp.stack(jnp.split(d_inputs_t, lax.axis_size('frame'), ax...]
    another operation x3, local copies, waits for them, and re-layouts: 6.68 us -> 1.12 us  [project_back(): flat_rows = matrix.reshape(-1, matrix.shape[-1])]
    unnamed x5, waiting for transfers between devices: 164 us -> 169 us
    dot_general x13, matrix products: 16.4 us -> 12.7 us  [cross(): lax.dot_general(left_rows, right_rows, (((0,), (0,)), ((), ())), preferre...]
    unnamed x44 -> x50, local copies, waits for them, and re-layouts: 10.5 us -> 9.67 us
  transfers between devices with their start and end apart: 10 -> 10, of which waited for: 8 -> 7; matrix products, arithmetic and copies ran while one was open for 15% -> 13% of each run, Pallas kernels for 0% -> 0%
where the time goes in v1:
time: 354 us; the launch traced here: 353 us
  waiting for transfers between devices  222 us (63%)
  local copies, waits for them, and re-layouts  41.8 us (12%)
  matrix products  35.2 us (10%)
  starting transfers between devices  28.1 us (8%)
  between operations  15 us (4%)
  other arithmetic  10.8 us (3%)
    unnamed x5, waiting for transfers between devices  169 us
    psum x1, waiting for transfers between devices, body(): summed = lax.psum(conv_term.astype(jnp.bfloat16), 'frame')  31.4 us
    dot_general x13, matrix products, cross(): lax.dot_general(left_rows, right_rows, (((0,), (0,)), ((), ())), preferre...  12.7 us
    all_to_all x1, waiting for transfers between devices, body(): lax.all_to_all(flat_x, 'frame', split_axis=2, concat_axis=1, tiled=True)  10 us
    unnamed x50, local copies, waits for them, and re-layouts  9.67 us
    dot_general x13, matrix products, project_back(): lax.dot_general(flat_rows, weight, (((1,), (1,)), ((), ())), preferred_el...  8.4 us
  transfers between devices with their start and end apart: 10, of which 7 were waited for; matrix products, arithmetic and copies ran while one was open for 13% of the time, Pallas kernels for 0%

profile of v1, /device:TPU:0, one launch (start us, length us, event | category | flops | bytes accessed | tf_op | source)
XLA Modules:
  0.0 352.9 jit_solution(10346924453671182730)
XLA Ops:
  7.2 0.7 convert_element_type.153
  8.0 0.8 copy.234
  8.8 6.3 %all-to-all-start.1 = ((bf16[1,2,256]{1,0,2:T(2,128)(2,1)}), bf16[1,2,256]{1,0,2:T(2,128)(2,1)S(1)}, u32[]{:S(2)}, u32[]{:S(2)}) async-start(bf16[1,2,256]{1,0,2:T(2,128)(2,1)} %copy.234), calls=%async_computation.1 | async-start | bytes 262144 | tf_op jit(solution)/shard_map/all_to_all | solution.py:64
  15.2 2.1 copy.222
  17.3 3.9 %all-to-all-done.1 = bf16[1,2,256]{1,0,2:T(2,128)(2,1)S(1)} async-done(((bf16[1,2,256]{1,0,2:T(2,128)(2,1)}), bf16[1,2,256]{1,0,2:T(2,128)(2,1)S(1)}, u32[]{:S(2)}, u32[]{:S(2)}) %all-to-all-start.1) | async-done | bytes 1056 | tf_op jit(solution)/shard_map/all_to_all | solution.py:64
  21.3 3.5 all-to-all-start
  25.1 10.0 %all-to-all-done = bf16[1,2,256,320]{3,1,0,2:T(2,128)(2,1)S(1)} async-done(((bf16[1,2,256,320]{3,1,0,2:T(2,128)(2,1)}), bf16[1,2,256,320]{3,1,0,2:T(2,128)(2,1)S(1)}, u32[]{:S(2)}, u32[]{:S(2)}) %all-to-all-start) | async-done | bytes 327712 | tf_op jit(solution)/shard_map/all_to_all | solution.py:63
  36.2 1.2 convolution_convert_fusion.4
  38.8 1.6 copy.226
  40.3 1.2 copy.238
  41.5 2.2 fusion.59
  43.7 0.7 copy-done.18
  44.4 2.7 fusion.7
  47.1 1.6 copy.240
  48.7 1.0 copy.241
  49.7 3.6 %all-to-all-start.2 = ((bf16[1,8,64,320]{3,2,0,1:T(8,128)(2,1)}), bf16[1,8,64,320]{3,2,0,1:T(8,128)(2,1)S(1)}, u32[]{:S(2)}, u32[]{:S(2)}) async-start(bf16[1,8,64,320]{3,2,0,1:T(8,128)(2,1)} %copy.241), calls=%async_computation.2 | async-start | bytes 786432 | tf_op jit(solution)/shard_map/all_to_all | solution.py:86
  53.4 1.0 copy.244
  54.4 0.9 copy.221
  56.5 6.7 %all-to-all-done.2 = bf16[1,8,64,320]{3,2,0,1:T(8,128)(2,1)S(1)} async-done(((bf16[1,8,64,320]{3,2,0,1:T(8,128)(2,1)}), bf16[1,8,64,320]{3,2,0,1:T(8,128)(2,1)S(1)}, u32[]{:S(2)}, u32[]{:S(2)}) %all-to-all-start.2) | async-done | bytes 327712 | tf_op jit(solution)/shard_map/all_to_all | solution.py:86
  63.3 2.3 multiply_convert_fusion.2
  65.9 1.4 collective-permute-start.1
  67.3 4.7 %collective-permute-start = (bf16[1,2,1,16,640]{4,3,2,1,0:T(8,128)(2,1)S(1)}, bf16[1,2,1,16,640]{4,3,2,1,0:T(8,128)(2,1)S(1)}, u32[]{:S(2)}, u32[]{:S(2)}) collective-permute-start(bf16[1,2,1,16,640]{4,3,2,1,0:T(8,128)(2,1)S(1)} %get-tuple-element.29), channel_id=1, source_target_pairs={{0,2},{2,4},{4,6},{1,3},{3,5},{5,7},{8,10},{10,12},{12,14},{9,11},... | collective-permute-start | bytes 122888 | tf_op jit(solution)/shard_map/ppermute | solution.py:14
  72.6 1.0 collective-permute-done
  73.6 0.8 select_maximum_fusion
  74.4 0.8 fusion.58
  75.2 1.2 convolution_bitcast_fusion.8
  76.9 1.2 convolution_bitcast_fusion.7
  78.0 1.2 convolution_bitcast_fusion.6
  79.2 1.2 convolution_bitcast_fusion.5
  80.4 1.2 convolution_bitcast_fusion.3
  81.6 1.2 convolution_bitcast_fusion.2
  83.0 1.2 convolution_bitcast_fusion.1
  84.2 1.2 convolution_bitcast_fusion
  90.5 0.8 reshape.301
  91.3 2.0 copy.247
  93.3 3.5 all-to-all-start.3
  97.1 4.9 %concatenate.29 = f32[2880,320]{0,1:T(8,128)} concatenate(f32[320,320]{0,1:T(8,128)} %convolution_bitcast_fusion.8, f32[320,320]{0,1:T(8,128)} %convolution_bitcast_fusion.7, f32[320,320]{0,1:T(8,128)} %convolution_bitcast_fusion.6, f32[320,320]{0,1:T(8,128)} %convolution_bitcast_fusion.5, f32[320,320]{0,1:T(8,128)S(1)} %convolution_bitcast_fusion.4, ...), dimensions={0} | concatenate | bytes 7372800 | tf_op jit(solution)/shard_map/concatenate | solution.py:183
  102.0 3.6 %multiply_convert_fusion = bf16[2880,320]{0,1:T(8,128)(2,1)} fusion(f32[2880,320]{0,1:T(8,128)} %concatenate.29), kind=kLoop, calls=%fused_computation.1 | loop fusion | flops 1843200 | bytes 5529600 | tf_op jit(solution)/shard_map/convert_element_type | solution.py:184
  105.6 1.1 fusion.60
  107.1 1.2 copy.250
  108.4 2.4 multiply_reduce_fusion
  112.6 0.6 copy-done.15
  113.2 1.4 fusion.8
  114.6 1.3 copy.254
  115.9 1.6 fusion.34
  117.4 1.3 copy.257
  118.7 2.4 copy.260
  121.1 1.7 convolution_add_fusion.1
  123.3 0.7 slice_bitcast_fusion.19
  126.1 0.8 pad_maximum_fusion.1
  126.9 4.8 %all-to-all-start.4 = ((bf16[4,1,2,64,320]{4,3,2,1,0:T(8,128)(2,1)}), bf16[4,1,2,64,320]{4,3,2,1,0:T(8,128)(2,1)}, u32[]{:S(2)}, u32[]{:S(2)}) async-start(bf16[4,1,2,64,320]{4,3,2,1,0:T(8,128)(2,1)} %pad_maximum_fusion.1), calls=%async_computation.4 | async-start | bytes 786432 | tf_op jit(solution)/shard_map/all_to_all | solution.py:160
  133.5 1.1 convolution_bitcast_fusion.9
  134.7 1.5 concatenate.28
  136.2 32.9 %all-reduce.11.cloned.1.call-done = bf16[2880,320]{0,1:T(8,128)(2,1)} async-done(((bf16[2880,320]{0,1:T(8,128)(2,1)}), bf16[2880,320]{0,1:T(8,128)(2,1)}) %all-reduce.11.cloned.1.call-update) | async-done | bytes 1843216
  169.1 1.8 constant_dynamic-slice_fusion
  170.9 1.3 broadcast_multiply_fusion
  172.2 1.1 convert_bitcast_fusion
  173.6 0.6 copy-done.3
  174.4 0.9 copy.264
  175.3 31.4 %all-reduce.7.cloned.1.call-done = bf16[360,320]{0,1:T(8,128)(2,1)} async-done(((bf16[360,320]{0,1:T(8,128)(2,1)}), bf16[360,320]{0,1:T(8,128)(2,1)}) %all-reduce.7.cloned.1.call-update) | async-done | bytes 230416 | tf_op jit(solution)/shard_map/psum | solution.py:184
  206.7 1.8 convert_element_type.185
  208.5 136.1 %all-reduce.9.cloned.1.call-done = f32[1280,320]{0,1:T(8,128)} async-done(((f32[1280,320]{0,1:T(8,128)}), f32[1280,320]{0,1:T(8,128)}) %all-reduce.9.cloned.1.call-update) | async-done | bytes 1638416
  344.6 1.1 constant_dynamic-slice_fusion.1
  345.7 0.7 copy.271
  (101 shorter events, 17.4 us)
Async XLA Ops:
  7.2 17.6 %copy-start.20 = (f32[5,8,8]{2,1,0:T(8,128)S(1)}, f32[5,8,8]{2,1,0:T(8,128)}, u32[]{:S(2)}) copy-start(f32[5,8,8]{2,1,0:T(8,128)} %param.11) | copy-start | bytes 3844
  8.8 12.4 %all-to-all-start.1 = ((bf16[1,2,256]{1,0,2:T(2,128)(2,1)}), bf16[1,2,256]{1,0,2:T(2,128)(2,1)S(1)}, u32[]{:S(2)}, u32[]{:S(2)}) async-start(bf16[1,2,256]{1,0,2:T(2,128)(2,1)} %copy.234), calls=%async_computation.1 | async-start | bytes 262144 | tf_op jit(solution)/shard_map/all_to_all | solution.py:64
  17.3 17.9 %copy-start.1 = (bf16[1280,320]{0,1:T(8,128)(2,1)S(1)}, bf16[1280,320]{0,1:T(8,128)(2,1)}, u32[]{:S(2)}) copy-start(bf16[1280,320]{0,1:T(8,128)(2,1)} %param.9) | copy-start | bytes 2457604
  21.3 13.9 %all-to-all-start = ((bf16[1,2,256,320]{3,1,0,2:T(2,128)(2,1)}), bf16[1,2,256,320]{3,1,0,2:T(2,128)(2,1)S(1)}, u32[]{:S(2)}, u32[]{:S(2)}) async-start(bf16[1,2,256,320]{3,1,0,2:T(2,128)(2,1)} %bitcast.2), calls=%async_computation | async-start | bytes 786432 | tf_op jit(solution)/shard_map/all_to_all | solution.py:63
  38.8 4.9 %copy-start.6 = (bf16[8,64,5,64]{3,0,2,1:T(8,128)(2,1)}, bf16[8,64,5,64]{3,0,2,1:T(8,128)(2,1)S(1)}, u32[]{:S(2)}) copy-start(bf16[8,64,5,64]{3,0,2,1:T(8,128)(2,1)S(1)} %copy.231) | copy-start | bytes 983044
  41.5 2.9 copy-start.12
  43.7 0.7 copy-start.18
  47.1 6.2 %copy-start.10 = (bf16[1,2,16,16,320]{4,3,2,1,0:T(8,128)(2,1)S(1)}, bf16[1,2,16,16,320]{4,3,2,1,0:T(8,128)(2,1)}, u32[]{:S(2)}) copy-start(bf16[1,2,16,16,320]{4,3,2,1,0:T(8,128)(2,1)} %param.6) | copy-start | bytes 983044
  48.7 5.7 %copy-start = (bf16[1,2,16,16,320]{4,3,2,1,0:T(8,128)(2,1)S(1)}, bf16[1,2,16,16,320]{4,3,2,1,0:T(8,128)(2,1)}, u32[]{:S(2)}) copy-start(bf16[1,2,16,16,320]{4,3,2,1,0:T(8,128)(2,1)} %param.7) | copy-start | bytes 983044
  49.7 5.6 %copy-start.21 = (u32[32]{0:T(128)S(1)}, u32[32]{0:T(128)}, u32[]{:S(2)}) copy-start(u32[32]{0:T(128)} %constant.30) | copy-start | bytes 388
  49.7 13.5 %all-to-all-start.2 = ((bf16[1,8,64,320]{3,2,0,1:T(8,128)(2,1)}), bf16[1,8,64,320]{3,2,0,1:T(8,128)(2,1)S(1)}, u32[]{:S(2)}, u32[]{:S(2)}) async-start(bf16[1,8,64,320]{3,2,0,1:T(8,128)(2,1)} %copy.241), calls=%async_computation.2 | async-start | bytes 786432 | tf_op jit(solution)/shard_map/all_to_all | solution.py:86
  65.8 6.7 %copy-start.14 = (f32[2,256,320]{1,2,0:T(8,128)S(1)}, f32[2,256,320]{1,2,0:T(8,128)}, u32[]{:S(2)}) copy-start(f32[2,256,320]{1,2,0:T(8,128)} %get-tuple-element.38) | copy-start | bytes 1966084
  65.9 6.6 %collective-permute-start.1 = (bf16[1,2,1,16,640]{4,3,2,1,0:T(8,128)(2,1)S(1)}, bf16[1,2,1,16,640]{4,3,2,1,0:T(8,128)(2,1)S(1)}, u32[]{:S(2)}, u32[]{:S(2)}) collective-permute-start(bf16[1,2,1,16,640]{4,3,2,1,0:T(8,128)(2,1)S(1)} %get-tuple-element.30), channel_id=1, source_target_pairs={{2,0},{4,2},{6,4},{3,1},{5,3},{7,5},{10,8},{12,10},{14,12},{11,9},... | collective-permute-start | bytes 122888 | tf_op jit(solution)/shard_map/ppermute | solution.py:17
  67.3 6.2 %collective-permute-start = (bf16[1,2,1,16,640]{4,3,2,1,0:T(8,128)(2,1)S(1)}, bf16[1,2,1,16,640]{4,3,2,1,0:T(8,128)(2,1)S(1)}, u32[]{:S(2)}, u32[]{:S(2)}) collective-permute-start(bf16[1,2,1,16,640]{4,3,2,1,0:T(8,128)(2,1)S(1)} %get-tuple-element.29), channel_id=1, source_target_pairs={{0,2},{2,4},{4,6},{1,3},{3,5},{5,7},{8,10},{10,12},{12,14},{9,11},... | collective-permute-start | bytes 122888 | tf_op jit(solution)/shard_map/ppermute | solution.py:14
  83.0 2.4 copy-start.8
  88.5 1.0 copy-start.17
  90.0 15.6 %copy-start.2 = (bf16[512,320]{0,1:T(8,128)(2,1)}, bf16[512,320]{0,1:T(8,128)(2,1)S(1)}, u32[]{:S(2)}) copy-start(bf16[512,320]{0,1:T(8,128)(2,1)S(1)} %fusion.15) | copy-start | bytes 983044
  93.3 13.4 %all-to-all-start.3 = ((bf16[1,2,256,320]{3,1,0,2:T(2,128)(2,1)}), bf16[1,2,256,320]{3,1,0,2:T(2,128)(2,1)S(1)}, u32[]{:S(2)}, u32[]{:S(2)}) async-start(bf16[1,2,256,320]{3,1,0,2:T(2,128)(2,1)} %copy.247), calls=%async_computation.3 | async-start | bytes 786432 | tf_op jit(solution)/shard_map/all_to_all | solution.py:129
  96.8 72.3 %all-reduce.11.cloned.1.call-start = ((), (), s32[]{:S(2)}) async-start(), calls=%async_computation.7 | async-start | bytes 3768320
  106.7 1.6 copy-start.19
  107.1 1.3 copy-start.13
  108.4 2.4 copy-start.11
  111.0 1.1 copy-start.7
  112.1 1.1 copy-start.15
  121.1 1.7 copy-start.5
  124.0 1.2 copy-start.4
  125.2 0.9 copy-start.16
  126.9 45.3 %all-to-all-start.4 = ((bf16[4,1,2,64,320]{4,3,2,1,0:T(8,128)(2,1)}), bf16[4,1,2,64,320]{4,3,2,1,0:T(8,128)(2,1)}, u32[]{:S(2)}, u32[]{:S(2)}) async-start(bf16[4,1,2,64,320]{4,3,2,1,0:T(8,128)(2,1)} %pad_maximum_fusion.1), calls=%async_computation.4 | async-start | bytes 786432 | tf_op jit(solution)/shard_map/all_to_all | solution.py:160
  131.7 75.0 %all-reduce.7.cloned.1.call-start = ((), (), s32[]{:S(2)}) async-start(), calls=%async_computation.5 | async-start | bytes 491520 | tf_op jit(solution)/shard_map/psum | solution.py:184
  133.2 1.5 copy-start.9
  170.9 173.7 %all-reduce.9.cloned.1.call-start = ((), (), s32[]{:S(2)}) async-start(), calls=%async_computation.6 | async-start | bytes 3276800
  173.3 1.0 copy-start.3
Sparse Core Ops, SparseCore 0:
  105.7 63.3 all-reduce.10
  172.0 34.7 all-reduce.6
  212.1 132.4 all-reduce.8
